TPU v7x, 32 devices: a whole 2x2x4 slice. The times are simulated.
32 devices in a mesh: band: 8 (over z, y), grid: 4 (over x, core).
Axes of the slice: x: 2, y: 2, z: 4, core: 2. Of those that a mesh axis runs over, the one named last changes fastest.
Arguments:
- own_bands: float32 [32, 128, 128, 128], P('band', 'grid'), may hold values from -1.5 to 1.5
- travel_bands: float32 [32, 128, 128, 128], P('band', 'grid'), may hold values from -1.5 to 1.5
Outputs:
- own_terms: float32 [32, 128, 128, 128], P('band', 'grid')
- partner_terms: float32 [32, 128, 128, 128], P('band', 'grid')
All inputs are finite; a program needn't handle non-finite values.
Results may differ from a plain program's by a relative error of at most 0.00011.
Values sent between devices are 32-bit elements; how exact they have to be, the bound alone decides.
A program may use at most 192 MiB of HBM per device.

v0:
```python
import math

import jax
import jax.numpy as jnp
from jax import lax
from jax.sharding import PartitionSpec as P

NX = 128
NY = 128
NZ = 128


FRACTION = 0.25
HIGHEST_PRECISION = lax.Precision.HIGHEST


def passed_along(block, axis, distance):
    devices = range(lax.axis_size(axis))
    route = [((i - distance) % len(devices), i) for i in devices]
    return lax.ppermute(block, axis, route)


def wave_square(points, first_row, length):
    position = first_row + jnp.arange(points, dtype=jnp.int32)
    position = (position + length // 2) % length - length // 2
    wavenumber = 2.0 * math.pi / length * position.astype(jnp.float32)
    return wavenumber * wavenumber


def coulomb(first_row, row_count):
    squared = (
        wave_square(NZ, 0, NZ)[:, None, None]
        + wave_square(row_count, first_row, NY)[None, :, None]
        + wave_square(NX, 0, NX)[None, None, :]
    )
    safe_square = jnp.where(squared > 0.0, squared, 1.0)
    return jnp.where(squared > 0.0, 4.0 * math.pi / safe_square, 0.0)


def fourier_table(length, inverse):
    position = jnp.arange(length, dtype=jnp.int32)
    phase_turns = position[:, None] * position[None, :] % length
    phase_angle = 2.0 * math.pi / length * phase_turns.astype(jnp.float32)
    cosine = jnp.cos(phase_angle)
    sine_part = jnp.sin(phase_angle)
    norm_factor = 1.0
    if inverse:
        sine_part = -sine_part
        norm_factor = 1.0 / length
    return norm_factor * jnp.stack(
        [jnp.stack([cosine, -sine_part]), jnp.stack([sine_part, cosine])]
    )


def solve_pairs(packed, kernel_slab):
    spectrum = jnp.einsum(
        "pczyx,cdxk->dpzyk", packed, fourier_table(NX, False), precision=HIGHEST_PRECISION
    )
    spectrum = jnp.einsum(
        "cpzyx,cdyk->dpzkx", spectrum, fourier_table(NY, False), precision=HIGHEST_PRECISION
    )
    forward_z = fourier_table(NZ, False)
    inverse_z = fourier_table(NZ, True)
    screened = (
        jnp.einsum(
            "cpzyx,cdzk->dpkyx",
            lax.all_to_all(spectrum, "grid", split_axis=3, concat_axis=2, tiled=True),
            forward_z,
            precision=HIGHEST_PRECISION,
        )
        * kernel_slab
    )
    screened = jnp.einsum("cpzyx,cdzk->dpkyx", screened, inverse_z, precision=HIGHEST_PRECISION)
    planes = lax.all_to_all(screened, "grid", split_axis=2, concat_axis=3, tiled=True)
    planes = jnp.einsum(
        "cpzyx,cdyk->dpzkx", planes, fourier_table(NY, True), precision=HIGHEST_PRECISION
    )
    return jnp.einsum(
        "cpzyx,cdxk->pdzyk", planes, fourier_table(NX, True), precision=HIGHEST_PRECISION
    )


def pair_terms(owned, visitors, kernel_slab):
    count_vis = visitors.shape[0]
    count_own = owned.shape[0]
    density = owned[None] * visitors[:, None]
    packed = density.reshape((count_vis * count_own // 2, 2) + owned.shape[1:])
    potential = solve_pairs(packed, kernel_slab).reshape(density.shape)
    own_part = jnp.sum(potential * visitors[:, None], axis=0)
    partner = jnp.sum(potential * owned[None], axis=1)
    return (own_part, partner)


def body(own_bands, travel_bands):
    rows_local = NY // lax.axis_size("grid")
    kernel_slab = coulomb(lax.axis_index("grid") * rows_local, rows_local)
    count_vis = travel_bands.shape[0]
    own_total = jnp.zeros_like(own_bands)
    returned = []
    for visit_index in range(count_vis):
        visitor = passed_along(travel_bands[visit_index : visit_index + 1], "band", 1)
        own_part, partner = pair_terms(own_bands, visitor, kernel_slab)
        own_total = own_total + own_part
        returned.append(passed_along(partner, "band", -1))
    partner_total = jnp.concatenate(returned, axis=0)
    return (-FRACTION * own_total, -FRACTION * partner_total)


def solution(mesh):
    in_specs = (P("band", "grid", None, None), P("band", "grid", None, None))
    out_specs = (P("band", "grid", None, None), P("band", "grid", None, None))
    return jax.shard_map(body, mesh=mesh, in_specs=in_specs, out_specs=out_specs, check_vma=False)
```

profile of v0, /device:TPU:0, one launch (start us, length us, event | category | flops | bytes accessed | tf_op | source)
XLA Modules:
  0.0 1270.8 jit_solution(9718589673150439641)
XLA Ops:
  12.9 44.4 %collective-permute-done = f32[1,32,128,128]{3,2,1,0:T(8,128)S(1)} collective-permute-done((f32[1,32,128,128]{3,2,1,0:T(8,128)S(1)}, f32[1,32,128,128]{3,2,1,0:T(8,128)S(1)}, u32[]{:S(2)}, u32[]{:S(2)}) %collective-permute-start) | collective-permute-done | bytes 2097184 | tf_op jit(solution)/shard_map/ppermute | solution.py:20
  57.3 45.0 %collective-permute-done.1 = f32[1,32,128,128]{3,2,1,0:T(8,128)} collective-permute-done((f32[1,32,128,128]{3,2,1,0:T(8,128)S(1)}, f32[1,32,128,128]{3,2,1,0:T(8,128)}, u32[]{:S(2)}, u32[]{:S(2)}) %collective-permute-start.1) | collective-permute-done | bytes 2097184 | tf_op jit(solution)/shard_map/ppermute | solution.py:20
  102.3 44.9 %collective-permute-done.3 = f32[1,32,128,128]{3,2,1,0:T(8,128)} collective-permute-done((f32[1,32,128,128]{3,2,1,0:T(8,128)S(1)}, f32[1,32,128,128]{3,2,1,0:T(8,128)}, u32[]{:S(2)}, u32[]{:S(2)}) %collective-permute-start.3) | collective-permute-done | bytes 2097184 | tf_op jit(solution)/shard_map/ppermute | solution.py:20
  147.2 44.1 %collective-permute-done.2 = f32[1,32,128,128]{3,2,1,0:T(8,128)} collective-permute-done((f32[1,32,128,128]{3,2,1,0:T(8,128)S(1)}, f32[1,32,128,128]{3,2,1,0:T(8,128)}, u32[]{:S(2)}, u32[]{:S(2)}) %collective-permute-start.2) | collective-permute-done | bytes 2097184 | tf_op jit(solution)/shard_map/ppermute | solution.py:20
  191.3 16.9 %broadcast_multiply_fusion.3 = (f32[4,32,128,128]{3,2,1,0:T(8,128)}, f32[4,32,128,128]{3,2,1,0:T(8,128)}, f32[4,32,128,128]{3,2,1,0:T(8,128)}, f32[4,32,128,128]{3,2,1,0:T(8,128)}) fusion(f32[4,32,128,128]{3,2,1,0:T(8,128)} %param.2, f32[32,128,128]{2,1,0:T(8,128)S(1)} %bitcast.406, f32[32,128,128]{2,1,0:T(8,128)} %bitcast.89, f32[32,128,128]{2,1,0:T(8,128)} %bitcast.51, ...), kind=kLoop, calls=%fused_computation.80 | loop fusion | flops 8388608 | bytes 50331648 | tf_op jit(solution)/shard_map/mul | solution.py:86
  208.2 9.6 fusion.45
  217.9 8.8 fusion.82
  226.7 8.7 copy.106
  235.4 5.6 all-to-all-start.4
  241.0 9.5 fusion.58
  250.5 8.8 fusion.76
  259.3 8.4 copy.78
  267.8 66.4 %all-to-all-done.4 = f32[2,2,32,128,128]{4,2,1,0,3:T(8,128)} async-done(((f32[2,2,32,128,128]{4,2,1,0,3:T(8,128)}), f32[2,2,32,128,128]{4,2,1,0,3:T(8,128)}, u32[]{:S(2)}, u32[]{:S(2)}) %all-to-all-start.4) | async-done | bytes 8388640 | tf_op jit(solution)/shard_map/all_to_all | solution.py:67
  334.2 5.7 all-to-all-start
  339.9 9.5 fusion.52
  349.3 8.8 fusion.79
  358.2 8.7 copy.92
  366.8 66.2 %all-to-all-done = f32[2,2,32,128,128]{4,2,1,0,3:T(8,128)} async-done(((f32[2,2,32,128,128]{4,2,1,0,3:T(8,128)}), f32[2,2,32,128,128]{4,2,1,0,3:T(8,128)}, u32[]{:S(2)}, u32[]{:S(2)}) %all-to-all-start) | async-done | bytes 8388640 | tf_op jit(solution)/shard_map/all_to_all | solution.py:67
  438.7 9.5 fusion.38
  448.1 8.8 fusion.85
  457.0 8.4 copy.120
  465.4 66.4 %all-to-all-done.2 = f32[2,2,32,128,128]{4,2,1,0,3:T(8,128)} async-done(((f32[2,2,32,128,128]{4,2,1,0,3:T(8,128)}), f32[2,2,32,128,128]{4,2,1,0,3:T(8,128)}, u32[]{:S(2)}, u32[]{:S(2)}) %all-to-all-start.2) | async-done | bytes 8388640 | tf_op jit(solution)/shard_map/all_to_all | solution.py:67
  531.8 5.7 all-to-all-start.6
  538.2 9.9 copy.108
  548.1 12.7 fusion.43
  560.8 9.2 fusion.70
  570.0 8.3 copy.111
  578.3 52.4 %all-to-all-done.6 = f32[2,2,32,128,128]{4,2,1,0,3:T(8,128)} async-done(((f32[2,2,32,128,128]{4,2,1,0,3:T(8,128)}), f32[2,2,32,128,128]{4,2,1,0,3:T(8,128)}, u32[]{:S(2)}, u32[]{:S(2)}) %all-to-all-start.6) | async-done | bytes 8388640 | tf_op jit(solution)/shard_map/all_to_all | solution.py:67
  630.6 5.8 all-to-all-start.5
  636.5 9.9 copy.80
  646.3 12.7 fusion.56
  659.0 9.2 fusion.64
  668.2 8.3 copy.83
  676.5 52.9 %all-to-all-done.5 = f32[2,2,128,32,128]{4,3,1,0,2:T(8,128)} async-done(((f32[2,2,128,32,128]{4,3,1,0,2:T(8,128)}), f32[2,2,128,32,128]{4,3,1,0,2:T(8,128)}, u32[]{:S(2)}, u32[]{:S(2)}) %all-to-all-start.5) | async-done | bytes 8388640 | tf_op jit(solution)/shard_map/all_to_all | solution.py:74
  729.4 5.9 all-to-all-start.1
  735.3 9.9 copy.94
  745.2 12.7 fusion.50
  757.9 9.2 fusion.67
  767.1 8.3 copy.97
  775.3 52.9 %all-to-all-done.1 = f32[2,2,128,32,128]{4,3,1,0,2:T(8,128)} async-done(((f32[2,2,128,32,128]{4,3,1,0,2:T(8,128)}), f32[2,2,128,32,128]{4,3,1,0,2:T(8,128)}, u32[]{:S(2)}, u32[]{:S(2)}) %all-to-all-start.1) | async-done | bytes 8388640 | tf_op jit(solution)/shard_map/all_to_all | solution.py:74
  828.3 5.8 all-to-all-start.3
  834.1 9.9 copy.122
  844.0 12.7 fusion.36
  856.7 9.2 fusion.73
  865.9 8.1 copy.125
  874.0 53.1 %all-to-all-done.3 = f32[2,2,128,32,128]{4,3,1,0,2:T(8,128)} async-done(((f32[2,2,128,32,128]{4,3,1,0,2:T(8,128)}), f32[2,2,128,32,128]{4,3,1,0,2:T(8,128)}, u32[]{:S(2)}, u32[]{:S(2)}) %all-to-all-start.3) | async-done | bytes 8388640 | tf_op jit(solution)/shard_map/all_to_all | solution.py:74
  927.1 5.9 all-to-all-start.7
  937.3 8.6 fusion.10
  945.9 10.5 fusion.94
  956.4 9.0 copy.117
  969.8 8.6 fusion.14
  978.4 10.7 fusion.88
  989.1 8.9 copy.89
  1002.5 8.6 fusion.12
  1011.0 10.4 fusion.91
  1021.5 9.0 copy.103
  1034.9 8.6 fusion.8
  1043.5 10.5 fusion.97
  1053.9 9.1 copy.131
  1063.1 20.9 %fusion.54 = (f32[32,128,128]{2,1,0:T(8,128)S(1)}, f32[32,128,128]{2,1,0:T(8,128)S(1)}, f32[32,128,128]{2,1,0:T(8,128)S(1)}, f32[32,128,128]{2,1,0:T(8,128)S(1)}, f32[4,32,128,128]{3,2,1,0:T(8,128)}) fusion(f32[4,32,128,128]{3,2,1,0:T(8,128)} %param.2, f32[2,2,32,128,128]{4,3,2,1,0:T(8,128)} %copy.89, f32[2,2,32,128,128]{4,3,2,1,0:T(8,128)} %copy.103, ...), kind=kLoop, calls=%fused_computation.66 | loop fusion | flops 31457280 | bytes 67108864 | tf_op jit(solution)/shard_map/reduce_sum | solution.py:90
  1089.0 43.4 %collective-permute-done.5 = f32[1,32,128,128]{3,2,1,0:T(8,128)S(1)} collective-permute-done((f32[1,32,128,128]{3,2,1,0:T(8,128)S(1)}, f32[1,32,128,128]{3,2,1,0:T(8,128)S(1)}, u32[]{:S(2)}, u32[]{:S(2)}) %collective-permute-start.5) | collective-permute-done | bytes 2097184 | tf_op jit(solution)/shard_map/ppermute | solution.py:20
  1132.5 44.9 %collective-permute-done.4 = f32[1,32,128,128]{3,2,1,0:T(8,128)S(1)} collective-permute-done((f32[1,32,128,128]{3,2,1,0:T(8,128)S(1)}, f32[1,32,128,128]{3,2,1,0:T(8,128)S(1)}, u32[]{:S(2)}, u32[]{:S(2)}) %collective-permute-start.4) | collective-permute-done | bytes 2097184 | tf_op jit(solution)/shard_map/ppermute | solution.py:20
  1177.4 44.9 %collective-permute-done.7 = f32[1,32,128,128]{3,2,1,0:T(8,128)S(1)} collective-permute-done((f32[1,32,128,128]{3,2,1,0:T(8,128)S(1)}, f32[1,32,128,128]{3,2,1,0:T(8,128)S(1)}, u32[]{:S(2)}, u32[]{:S(2)}) %collective-permute-start.7) | collective-permute-done | bytes 2097184 | tf_op jit(solution)/shard_map/ppermute | solution.py:20
  1222.4 44.4 %collective-permute-done.6 = f32[1,32,128,128]{3,2,1,0:T(8,128)S(1)} collective-permute-done((f32[1,32,128,128]{3,2,1,0:T(8,128)S(1)}, f32[1,32,128,128]{3,2,1,0:T(8,128)S(1)}, u32[]{:S(2)}, u32[]{:S(2)}) %collective-permute-start.6) | collective-permute-done | bytes 2097184 | tf_op jit(solution)/shard_map/ppermute | solution.py:20
  (27 shorter events, 45.0 us)
Async XLA Ops:
  4.7 52.6 %collective-permute-start = (f32[1,32,128,128]{3,2,1,0:T(8,128)S(1)}, f32[1,32,128,128]{3,2,1,0:T(8,128)S(1)}, u32[]{:S(2)}, u32[]{:S(2)}) collective-permute-start(f32[1,32,128,128]{3,2,1,0:T(8,128)S(1)} %get-tuple-element.11), channel_id=1, source_target_pairs={{28,0},{0,4},{4,8},{8,12},{12,16},{16,20},{20,24},{24,28},{29,1},{... | collective-permute-start | bytes 6291464 | tf_op jit(solution)/shard_map/ppermute | solution.py:20
  7.7 94.6 %collective-permute-start.1 = (f32[1,32,128,128]{3,2,1,0:T(8,128)S(1)}, f32[1,32,128,128]{3,2,1,0:T(8,128)}, u32[]{:S(2)}, u32[]{:S(2)}) collective-permute-start(f32[1,32,128,128]{3,2,1,0:T(8,128)S(1)} %get-tuple-element.12), channel_id=1, source_target_pairs={{28,0},{0,4},{4,8},{8,12},{12,16},{16,20},{20,24},{24,28},{29,1},{... | collective-permute-start | bytes 6291464 | tf_op jit(solution)/shard_map/ppermute | solution.py:20
  9.3 138.0 %collective-permute-start.3 = (f32[1,32,128,128]{3,2,1,0:T(8,128)S(1)}, f32[1,32,128,128]{3,2,1,0:T(8,128)}, u32[]{:S(2)}, u32[]{:S(2)}) collective-permute-start(f32[1,32,128,128]{3,2,1,0:T(8,128)S(1)} %get-tuple-element.13), channel_id=1, source_target_pairs={{28,0},{0,4},{4,8},{8,12},{12,16},{16,20},{20,24},{24,28},{29,1},{... | collective-permute-start | bytes 6291464 | tf_op jit(solution)/shard_map/ppermute | solution.py:20
  10.8 180.6 %collective-permute-start.2 = (f32[1,32,128,128]{3,2,1,0:T(8,128)S(1)}, f32[1,32,128,128]{3,2,1,0:T(8,128)}, u32[]{:S(2)}, u32[]{:S(2)}) collective-permute-start(f32[1,32,128,128]{3,2,1,0:T(8,128)S(1)} %get-tuple-element.14), channel_id=1, source_target_pairs={{28,0},{0,4},{4,8},{8,12},{12,16},{16,20},{20,24},{24,28},{29,1},{... | collective-permute-start | bytes 6291464 | tf_op jit(solution)/shard_map/ppermute | solution.py:20
  57.2 151.0 %copy-start = (f32[1,32,128,128]{3,2,1,0:T(8,128)}, f32[1,32,128,128]{3,2,1,0:T(8,128)S(1)}, u32[]{:S(2)}) copy-start(f32[1,32,128,128]{3,2,1,0:T(8,128)S(1)} %collective-permute-done) | copy-start | bytes 6291460
  235.4 98.8 %all-to-all-start.4 = ((f32[2,2,32,128,128]{4,2,1,0,3:T(8,128)}), f32[2,2,32,128,128]{4,2,1,0,3:T(8,128)}, u32[]{:S(2)}, u32[]{:S(2)}) async-start(f32[2,2,32,128,128]{4,2,1,0,3:T(8,128)} %copy.106), calls=%async_computation.4 | async-start | bytes 16777216 | tf_op jit(solution)/shard_map/all_to_all | solution.py:67
  334.2 98.8 %all-to-all-start = ((f32[2,2,32,128,128]{4,2,1,0,3:T(8,128)}), f32[2,2,32,128,128]{4,2,1,0,3:T(8,128)}, u32[]{:S(2)}, u32[]{:S(2)}) async-start(f32[2,2,32,128,128]{4,2,1,0,3:T(8,128)} %copy.78), calls=%async_computation | async-start | bytes 16777216 | tf_op jit(solution)/shard_map/all_to_all | solution.py:67
  433.0 98.8 %all-to-all-start.2 = ((f32[2,2,32,128,128]{4,2,1,0,3:T(8,128)}), f32[2,2,32,128,128]{4,2,1,0,3:T(8,128)}, u32[]{:S(2)}, u32[]{:S(2)}) async-start(f32[2,2,32,128,128]{4,2,1,0,3:T(8,128)} %copy.92), calls=%async_computation.2 | async-start | bytes 16777216 | tf_op jit(solution)/shard_map/all_to_all | solution.py:67
  531.8 98.8 %all-to-all-start.6 = ((f32[2,2,32,128,128]{4,2,1,0,3:T(8,128)}), f32[2,2,32,128,128]{4,2,1,0,3:T(8,128)}, u32[]{:S(2)}, u32[]{:S(2)}) async-start(f32[2,2,32,128,128]{4,2,1,0,3:T(8,128)} %copy.120), calls=%async_computation.6 | async-start | bytes 16777216 | tf_op jit(solution)/shard_map/all_to_all | solution.py:67
  630.6 98.8 %all-to-all-start.5 = ((f32[2,2,128,32,128]{4,3,1,0,2:T(8,128)}), f32[2,2,128,32,128]{4,3,1,0,2:T(8,128)}, u32[]{:S(2)}, u32[]{:S(2)}) async-start(f32[2,2,128,32,128]{4,3,1,0,2:T(8,128)} %copy.111), calls=%async_computation.5 | async-start | bytes 16777216 | tf_op jit(solution)/shard_map/all_to_all | solution.py:74
  729.4 98.8 %all-to-all-start.1 = ((f32[2,2,128,32,128]{4,3,1,0,2:T(8,128)}), f32[2,2,128,32,128]{4,3,1,0,2:T(8,128)}, u32[]{:S(2)}, u32[]{:S(2)}) async-start(f32[2,2,128,32,128]{4,3,1,0,2:T(8,128)} %copy.83), calls=%async_computation.1 | async-start | bytes 16777216 | tf_op jit(solution)/shard_map/all_to_all | solution.py:74
  828.3 98.8 %all-to-all-start.3 = ((f32[2,2,128,32,128]{4,3,1,0,2:T(8,128)}), f32[2,2,128,32,128]{4,3,1,0,2:T(8,128)}, u32[]{:S(2)}, u32[]{:S(2)}) async-start(f32[2,2,128,32,128]{4,3,1,0,2:T(8,128)} %copy.97), calls=%async_computation.3 | async-start | bytes 16777216 | tf_op jit(solution)/shard_map/all_to_all | solution.py:74
  927.1 103.4 %all-to-all-start.7 = ((f32[2,2,128,32,128]{4,3,1,0,2:T(8,128)}), f32[2,2,128,32,128]{4,3,1,0,2:T(8,128)}, u32[]{:S(2)}, u32[]{:S(2)}) async-start(f32[2,2,128,32,128]{4,3,1,0,2:T(8,128)} %copy.125), calls=%async_computation.7 | async-start | bytes 16777216 | tf_op jit(solution)/shard_map/all_to_all | solution.py:74
  1053.9 9.1 copy-start.1
  1084.0 48.5 %collective-permute-start.5 = (f32[1,32,128,128]{3,2,1,0:T(8,128)S(1)}, f32[1,32,128,128]{3,2,1,0:T(8,128)S(1)}, u32[]{:S(2)}, u32[]{:S(2)}) collective-permute-start(f32[1,32,128,128]{3,2,1,0:T(8,128)S(1)} %bitcast.411), channel_id=1, source_target_pairs={{4,0},{8,4},{12,8},{16,12},{20,16},{24,20},{28,24},{0,28},{5,1},{9... | collective-permute-start | bytes 6291464 | tf_op jit(solution)/shard_map/ppermute | solution.py:20
  1085.7 91.7 %collective-permute-start.4 = (f32[1,32,128,128]{3,2,1,0:T(8,128)S(1)}, f32[1,32,128,128]{3,2,1,0:T(8,128)S(1)}, u32[]{:S(2)}, u32[]{:S(2)}) collective-permute-start(f32[1,32,128,128]{3,2,1,0:T(8,128)S(1)} %bitcast.410), channel_id=1, source_target_pairs={{4,0},{8,4},{12,8},{16,12},{20,16},{24,20},{28,24},{0,28},{5,1},{9... | collective-permute-start | bytes 6291464 | tf_op jit(solution)/shard_map/ppermute | solution.py:20
  1087.1 135.2 %collective-permute-start.7 = (f32[1,32,128,128]{3,2,1,0:T(8,128)S(1)}, f32[1,32,128,128]{3,2,1,0:T(8,128)S(1)}, u32[]{:S(2)}, u32[]{:S(2)}) collective-permute-start(f32[1,32,128,128]{3,2,1,0:T(8,128)S(1)} %bitcast.409), channel_id=1, source_target_pairs={{4,0},{8,4},{12,8},{16,12},{20,16},{24,20},{28,24},{0,28},{5,1},{9... | collective-permute-start | bytes 6291464 | tf_op jit(solution)/shard_map/ppermute | solution.py:20
  1087.6 179.2 %collective-permute-start.6 = (f32[1,32,128,128]{3,2,1,0:T(8,128)S(1)}, f32[1,32,128,128]{3,2,1,0:T(8,128)S(1)}, u32[]{:S(2)}, u32[]{:S(2)}) collective-permute-start(f32[1,32,128,128]{3,2,1,0:T(8,128)S(1)} %bitcast.408), channel_id=1, source_target_pairs={{4,0},{8,4},{12,8},{16,12},{20,16},{24,20},{28,24},{0,28},{5,1},{9... | collective-permute-start | bytes 6291464 | tf_op jit(solution)/shard_map/ppermute | solution.py:20
where the time goes:
time: 1280 us; the launch traced here: 1270 us
  waiting for transfers between devices  766 us (60%)
  matrix products  237 us (19%)
  local copies, waits for them, and re-layouts  164 us (13%)
  starting transfers between devices  58.7 us (5%)
  other arithmetic  42.8 us (3%)
    ppermute x8, waiting for transfers between devices, passed_along(): return lax.ppermute(block, axis, route)  356 us
    all_to_all x4, waiting for transfers between devices, solve_pairs(): lax.all_to_all(spectrum, 'grid', split_axis=3, concat_axis=2, tiled=True)  251 us
    all_to_all x4, waiting for transfers between devices, solve_pairs(): lax.all_to_all(screened, 'grid', split_axis=2, concat_axis=3, tiled=True)  159 us
    dot_general x4, matrix products, solve_pairs(): jnp.einsum('cpzyx,cdzk->dpkyx', lax.all_to_all(spectrum, 'grid', split_ax...  50.7 us
    dot_general x4, matrix products, solve_pairs(): jnp.einsum('cpzyx,cdxk->pdzyk', planes, fourier_table(NX, True), precisio...  42.2 us
    all_to_all x4, local copies, waits for them, and re-layouts, solve_pairs(): lax.all_to_all(spectrum, 'grid', split_axis=3, concat_axis=2, tiled=True)  39.5 us
    dot_general x4, matrix products, solve_pairs(): jnp.einsum('pczyx,cdxk->dpzyk', packed, fourier_table(NX, False), precisi...  38.1 us
    dot_general x4, matrix products, solve_pairs(): jnp.einsum('cpzyx,cdzk->dpkyx', screened, inverse_z, precision=HIGHEST_PR...  36.9 us
  transfers between devices with their start and end apart: 16, of which 15 were waited for; matrix products, arithmetic and copies ran while one was open for 27% of the time, Pallas kernels for 0%

commit v1 on v0

--- a/solution.py
+++ b/solution.py
@@ -106,7 +106,124 @@
     return (-FRACTION * own_total, -FRACTION * partner_total)
 
 
+def exchanged(block, bit):
+    devices = range(lax.axis_size("grid"))
+    return lax.ppermute(block, "grid", [(i, i ^ bit) for i in devices])
+
+
+def line_table(from_position, to_position, length, inverse):
+    phase_turns = from_position[:, None] * to_position[None, :] % length
+    phase_angle = 2.0 * math.pi / length * phase_turns.astype(jnp.float32)
+    cosine = jnp.cos(phase_angle)
+    sine_part = jnp.sin(phase_angle)
+    norm_factor = 1.0
+    if inverse:
+        sine_part = -sine_part
+        norm_factor = 1.0 / length
+    return norm_factor * jnp.stack(
+        [jnp.stack([cosine, -sine_part]), jnp.stack([sine_part, cosine])]
+    )
+
+
+def transform(equation, values, table):
+    return jnp.einsum(equation, values, table, precision=lax.Precision.HIGH)
+
+
+def square_body(own_bands, travel_bands):
+    rank = lax.axis_index("grid")
+    chip, core = rank // 2, rank % 2
+    half_own = own_bands.shape[0] // 2
+    half_vis = travel_bands.shape[0] // 2
+    depth, ny, nx = own_bands.shape[1:]
+    nz = depth * lax.axis_size("grid")
+
+    def planes(first, second):
+        steps = jnp.arange(depth, dtype=jnp.int32)
+        return jnp.concatenate([first * depth + steps, second * depth + steps])
+
+    every_z = jnp.arange(nz, dtype=jnp.int32)
+    every_y = jnp.arange(ny, dtype=jnp.int32)
+    every_x = jnp.arange(nx, dtype=jnp.int32)
+    piece_z = (planes(rank, rank ^ 1), planes(rank ^ 2, rank ^ 3))
+    forward_x = line_table(every_x, every_x, nx, False)
+    forward_y = line_table(every_y, every_y, ny, False)
+    inverse_x = line_table(every_x, every_x, nx, True)
+    inverse_y = line_table(every_y, every_y, ny, True)
+    forward_z = [line_table(z, every_z, nz, False) for z in piece_z]
+    inverse_z = [line_table(every_z, z, nz, True) for z in piece_z]
+    kernel_cube = coulomb(0, ny)
+
+    own_mine = lax.dynamic_slice_in_dim(own_bands, chip * half_own, half_own, 0)
+    own_away = lax.dynamic_slice_in_dim(own_bands, (1 - chip) * half_own, half_own, 0)
+    own_far = exchanged(own_away, 2)
+    owned = [
+        jnp.concatenate([block, exchanged(block, 1)], axis=1) for block in (own_mine, own_far)
+    ]
+
+    visitors = []
+    for k in range(half_vis):
+        mine = lax.dynamic_index_in_dim(travel_bands, core * half_vis + k, 0, keepdims=False)
+        away = lax.dynamic_index_in_dim(travel_bands, (1 - core) * half_vis + k, 0, keepdims=False)
+        away = passed_along(away, "band", 1)
+        mine = passed_along(mine, "band", 1)
+        away = exchanged(away, 1)
+        visitors.append(
+            [
+                jnp.concatenate([mine, away], axis=0),
+                jnp.concatenate([exchanged(mine, 2), exchanged(away, 2)], axis=0),
+            ]
+        )
+
+    own_sum = [0.0, 0.0]
+    held_mine, held_away = [], []
+    for k in range(half_vis):
+        spectrum = 0.0
+        for p in (0, 1):
+            part = owned[p] * visitors[k][p][None]
+            part = transform("czyx,cdxk->dzyk", part, forward_x)
+            part = transform("czyx,cdyk->dzkx", part, forward_y)
+            spectrum = spectrum + transform("czyx,cdzk->dkyx", part, forward_z[p])
+        spectrum = spectrum * kernel_cube
+        held = [None, None]
+        for p in (1, 0):
+            part = transform("czyx,cdzk->dkyx", spectrum, inverse_z[p])
+            part = transform("czyx,cdyk->dzkx", part, inverse_y)
+            part = transform("czyx,cdxk->dzyk", part, inverse_x)
+            held[p] = jnp.sum(part * owned[p], axis=0)
+            own_sum[p] = own_sum[p] + part * visitors[k][p][None]
+        held_near = -FRACTION * (held[0] + exchanged(held[1], 2))
+        held_mine.append(passed_along(held_near[:depth], "band", -1))
+        held_away.append(passed_along(exchanged(held_near[depth:], 1), "band", -1))
+
+    own_near, own_back = [
+        -FRACTION * (total[:, :depth] + exchanged(total[:, depth:], 1)) for total in own_sum
+    ]
+    own_back = exchanged(own_back, 2)
+    own_rows = jnp.where(
+        chip == 0,
+        jnp.concatenate([own_near, own_back], axis=0),
+        jnp.concatenate([own_back, own_near], axis=0),
+    )
+    held_rows = jnp.where(
+        core == 0, jnp.stack(held_mine + held_away), jnp.stack(held_away + held_mine)
+    )
+    return own_rows, held_rows
+
+
 def solution(mesh):
     in_specs = (P("band", "grid", None, None), P("band", "grid", None, None))
     out_specs = (P("band", "grid", None, None), P("band", "grid", None, None))
-    return jax.shard_map(body, mesh=mesh, in_specs=in_specs, out_specs=out_specs, check_vma=False)
+
+    def placed(own_bands, travel_bands):
+        group_own = own_bands.shape[0] // mesh.shape["band"]
+        group_vis = travel_bands.shape[0] // mesh.shape["band"]
+        square = mesh.shape["grid"] == 4 and group_own == 4 and group_vis % 2 == 0
+        return jax.shard_map(
+            square_body if square else body,
+            mesh=mesh,
+            in_specs=in_specs,
+            out_specs=out_specs,
+            check_vma=False,
+        )(own_bands, travel_bands)
+
+    return placed

time: 1280 us -> 996 us (0.78)
  waiting for transfers between devices: 766 us -> 546 us
  local copies, waits for them, and re-layouts: 164 us -> 88 us
  starting transfers between devices: 58.7 us -> 20.6 us
  matrix products: 237 us -> 271 us
  other arithmetic: 42.8 us -> 66.4 us
    all_to_all x8 -> x0, waiting for transfers between devices: 410 us -> none  [the longest x4 251 us: solve_pairs(): lax.all_to_all(spectrum, 'grid', split_axis=3, concat_axis=2, tiled=True)]
    ppermute x0 -> x16, waiting for transfers between devices: none -> 211 us  [exchanged(): return lax.ppermute(block, 'grid', [(i, i ^ bit) for i in devices])]
    transpose x12 -> x0, local copies, waits for them, and re-layouts: 103 us -> none  [the longest x4 36 us: solve_pairs(): jnp.einsum('cpzyx,cdxk->pdzyk', planes, fourier_table(NX, True), precisio...]
    all_to_all x8 -> x0, local copies, waits for them, and re-layouts: 57.1 us -> none  [the longest x4 39.5 us: solve_pairs(): lax.all_to_all(spectrum, 'grid', split_axis=3, concat_axis=2, tiled=True)]
    all_to_all x8 -> x0, starting transfers between devices: 46 us -> none  [the longest x4 23.4 us: solve_pairs(): lax.all_to_all(screened, 'grid', split_axis=2, concat_axis=3, tiled=True)]
    unnamed x4 -> x49, local copies, waits for them, and re-layouts: 0.01 us -> 35.6 us
    dot_general x24, matrix products: 237 us -> 271 us  [transform(): return jnp.einsum(equation, values, table, precision=lax.Precision.HIGH)]
    concatenate x0 -> x5, local copies, waits for them, and re-layouts: none -> 27.3 us  [the longest x2 11.3 us: square_body(): jnp.concatenate([exchanged(mine, 2), exchanged(away, 2)], axis=0)]
  transfers between devices with their start and end apart: 16 -> 24, of which waited for: 15 -> 12; matrix products, arithmetic and copies ran while one was open for 27% -> 21% of each run, Pallas kernels for 0% -> 0%
where the time goes in v1:
time: 996 us; the launch traced here: 992 us
  waiting for transfers between devices  546 us (55%)
  matrix products  271 us (27%)
  local copies, waits for them, and re-layouts  88 us (9%)
  other arithmetic  66.4 us (7%)
  starting transfers between devices  20.6 us (2%)
    ppermute x8, waiting for transfers between devices, passed_along(): return lax.ppermute(block, axis, route)  334 us
    dot_general x24, matrix products, transform(): return jnp.einsum(equation, values, table, precision=lax.Precision.HIGH)  271 us
    ppermute x16, waiting for transfers between devices, exchanged(): return lax.ppermute(block, 'grid', [(i, i ^ bit) for i in devices])  211 us
    unnamed x49, local copies, waits for them, and re-layouts  35.6 us
  transfers between devices with their start and end apart: 24, of which 12 were waited for; matrix products, arithmetic and copies ran while one was open for 21% of the time, Pallas kernels for 0%

profile of v1, /device:TPU:0, one launch (start us, length us, event | category | flops | bytes accessed | tf_op | source)
XLA Modules:
  0.0 992.3 jit_solution(15595370734278157015)
XLA Ops:
  0.7 8.0 constant_dynamic-slice_fusion.1
  8.6 5.7 copy.147
  14.3 3.0 collective-permute-start.4
  17.3 6.4 dynamic-slice_bitcast_fusion.3
  28.2 5.6 copy.146
  35.0 40.1 %collective-permute-done.1 = f32[32,128,128]{2,1,0:T(8,128)} collective-permute-done((f32[32,128,128]{2,1,0:T(8,128)}, f32[32,128,128]{2,1,0:T(8,128)}, u32[]{:S(2)}, u32[]{:S(2)}) %collective-permute-start.1) | collective-permute-done | bytes 2097184 | tf_op jit(solution)/shard_map/ppermute | solution.py:20
  75.7 44.4 %collective-permute-done.2 = f32[32,128,128]{2,1,0:T(8,128)} collective-permute-done((f32[32,128,128]{2,1,0:T(8,128)}, f32[32,128,128]{2,1,0:T(8,128)}, u32[]{:S(2)}, u32[]{:S(2)}) %collective-permute-start.2) | collective-permute-done | bytes 2097184 | tf_op jit(solution)/shard_map/ppermute | solution.py:20
  121.5 43.6 %collective-permute-done.9 = f32[32,128,128]{2,1,0:T(8,128)} collective-permute-done((f32[32,128,128]{2,1,0:T(8,128)}, f32[32,128,128]{2,1,0:T(8,128)}, u32[]{:S(2)}, u32[]{:S(2)}) %collective-permute-start.9) | collective-permute-done | bytes 2097184 | tf_op jit(solution)/shard_map/ppermute | solution.py:20
  165.3 6.5 fusion.14
  174.2 34.5 %collective-permute-done.8 = f32[32,128,128]{2,1,0:T(8,128)} collective-permute-done((f32[32,128,128]{2,1,0:T(8,128)S(1)}, f32[32,128,128]{2,1,0:T(8,128)}, u32[]{:S(2)}, u32[]{:S(2)}) %collective-permute-start.8) | collective-permute-done | bytes 2097184 | tf_op jit(solution)/shard_map/ppermute | solution.py:20
  210.7 4.7 pad_maximum_fusion.1
  215.5 5.6 copy.26
  221.1 4.7 pad_maximum_fusion.3
  225.8 5.6 copy.40
  233.4 7.8 fusion.50
  241.2 4.7 constant_dynamic-update-slice_fusion.1
  245.9 6.3 fusion.86
  252.2 5.2 fusion.60
  257.4 6.5 fusion.80
  263.9 83.5 %collective-permute-done.7 = f32[32,128,128]{2,1,0:T(8,128)} collective-permute-done((f32[32,128,128]{2,1,0:T(8,128)}, f32[32,128,128]{2,1,0:T(8,128)}, u32[]{:S(2)}, u32[]{:S(2)}) %collective-permute-start.7) | collective-permute-done | bytes 2097184 | tf_op jit(solution)/shard_map/ppermute | solution.py:111
  347.4 4.8 pad_maximum_fusion.2
  352.2 5.6 copy.31
  357.8 32.4 %collective-permute-done.12 = f32[32,128,128]{2,1,0:T(8,128)} collective-permute-done((f32[32,128,128]{2,1,0:T(8,128)}, f32[32,128,128]{2,1,0:T(8,128)}, u32[]{:S(2)}, u32[]{:S(2)}) %collective-permute-start.12) | collective-permute-done | bytes 2097184 | tf_op jit(solution)/shard_map/ppermute | solution.py:111
  390.2 4.8 pad_maximum_fusion.4
  395.0 5.7 copy.44
  400.6 4.8 constant_dynamic-update-slice_fusion
  405.5 6.9 fusion.46
  412.4 4.5 fusion.89
  416.9 6.9 fusion.56
  423.7 4.7 fusion.83
  428.4 16.3 %fusion.44 = f32[2,128,128,128,1]{3,1,4,2,0:T(8,128)} fusion(f32[2,64,128,128]{3,2,1,0:T(8,128)S(1)} %fusion.89, f32[1,2,64,128]{3,2,1,0:T(8,128)S(1)} %get-tuple-element.39, f32[1,2,64,128]{3,2,1,0:T(8,128)S(1)} %get-tuple-element.38), kind=kOutput, calls=%fused_computation.59 | convolution fusion | flops 3221258240 | bytes 25296896 | tf_op jit(solution)/shard_map/czyx,cdzk->dkyx/dot_general | solution.py:129
  444.7 16.2 %fusion.54 = f32[2,128,128,128,1]{3,1,4,2,0:T(8,128)} fusion(f32[2,64,128,128]{3,2,1,0:T(8,128)S(1)} %fusion.83, f32[1,2,64,128]{3,2,1,0:T(8,128)S(1)} %get-tuple-element.39, f32[1,2,64,128]{3,2,1,0:T(8,128)S(1)} %get-tuple-element.38), kind=kOutput, calls=%fused_computation.69 | convolution fusion | flops 3221258240 | bytes 25296896 | tf_op jit(solution)/shard_map/czyx,cdzk->dkyx/dot_general | solution.py:129
  460.9 23.2 %fusion.4 = f32[2,128,128,128]{3,1,2,0:T(8,128)} fusion(f32[2,128,128,128,1]{3,1,4,2,0:T(8,128)} %fusion.44, f32[128,128,128]{2,0,1:T(8,128)} %fusion.14, f32[2,64,128,128]{3,2,1,0:T(8,128)} %fusion.86, f32[1,2,64,128]{3,2,0,1:T(8,128)S(1)} %copy-done.13, f32[1,2,64,128]{3,2,0,1:T(8,128)S(1)} %copy-done.12), kind=kOutput, calls=%fused_computation.5 | convolution fusion | flops 3229646848 | bytes 50462720 | tf_op jit(solution)/shard_map/czyx,cdzk->dkyx/dot_general | solution.py:129
  484.1 22.9 %fusion.9 = f32[2,128,128,128]{3,1,2,0:T(8,128)} fusion(f32[2,128,128,128,1]{3,1,4,2,0:T(8,128)} %fusion.54, f32[128,128,128]{2,0,1:T(8,128)} %fusion.14, f32[2,64,128,128]{3,2,1,0:T(8,128)} %fusion.80, f32[1,2,64,128]{3,2,0,1:T(8,128)S(1)} %copy-done.13, f32[1,2,64,128]{3,2,0,1:T(8,128)S(1)} %copy-done.12), kind=kOutput, calls=%fused_computation.11 | convolution fusion | flops 3229646848 | bytes 50462720 | tf_op jit(solution)/shard_map/czyx,cdzk->dkyx/dot_general | solution.py:129
  507.0 12.1 %fusion.101 = f32[2,64,128,128,1]{3,1,2,0,4:T(8,128)} fusion(f32[2,128,128,128]{3,1,2,0:T(8,128)} %fusion.4, f32[1,2,128,64]{2,3,0,1:T(8,128)S(1)} %copy-done.15, f32[1,2,128,64]{2,3,0,1:T(8,128)S(1)} %copy-done.14), kind=kOutput, calls=%fused_computation.106 | convolution fusion | flops 3221291008 | bytes 25296896 | tf_op jit(solution)/shard_map/czyx,cdzk->dkyx/dot_general | solution.py:129
  520.6 9.3 fusion.95
  529.9 12.3 %fusion.38 = f32[2,128,64,128,1]{3,1,4,0,2:T(8,128)S(1)} fusion(f32[2,64,128,128,1]{3,1,2,0,4:T(8,128)} %fusion.101, f32[2,2,128,128]{2,3,1,0:T(8,128)S(1)} %copy-done.9), kind=kOutput, calls=%fused_computation.53 | convolution fusion | flops 3221225472 | bytes 17039360 | tf_op jit(solution)/shard_map/czyx,cdyk->dzkx/dot_general | solution.py:129
  542.2 13.9 %fusion.40 = f32[2,128,64,128,1]{3,1,4,0,2:T(8,128)} fusion(f32[2,64,128,128,1]{3,1,2,0,4:T(8,128)S(1)} %copy-done.5, f32[2,2,128,128]{2,3,1,0:T(8,128)S(1)} %copy-done.9), kind=kOutput, calls=%fused_computation.55 | convolution fusion | flops 3221225472 | bytes 17039360 | tf_op jit(solution)/shard_map/czyx,cdyk->dzkx/dot_general | solution.py:129
  556.2 6.3 fusion.24
  562.5 18.9 %fusion.36 = (f32[64,128,128]{1,2,0:T(8,128)}, f32[64,128,128]{1,2,0:T(8,128)}, f32[2,64,128,128]{2,3,1,0:T(8,128)}) fusion(f32[2,64,128,128]{2,3,1,0:T(8,128)S(1)} %bitcast.352, f32[2,128,64,128,1]{3,1,4,2,0:T(8,128)} %fusion.24, f32[64,128,128]{1,2,0:T(8,128)} %copy.44, f32[64,128,128]{1,2,0:T(8,128)} %copy.31, f32[2,128,64,128,1]{3,1,4,0,2:T(8,128)} %fusion.40, ...), kind=kOutput, calls=%fused_computation.49 | convolution fusion | flops 3233808384 | bytes 50593792 | tf_op jit(solution)/shard_map/czyx,cdxk->dzyk/dot_general | solution.py:129
  582.1 9.3 fusion.98
  591.4 9.5 fusion.92
  602.3 8.6 fusion.42
  610.9 4.6 slice.35
  615.5 6.3 fusion.28
  621.9 13.9 %fusion.52 = f32[2,128,64,128,1]{3,1,4,0,2:T(8,128)} fusion(f32[2,64,128,128,1]{3,1,2,0,4:T(8,128)S(1)} %fusion.92, f32[2,2,128,128]{2,3,1,0:T(8,128)S(1)} %copy-done.9), kind=kOutput, calls=%fused_computation.67 | convolution fusion | flops 3221225472 | bytes 17039360 | tf_op jit(solution)/shard_map/czyx,cdyk->dzkx/dot_general | solution.py:129
  635.7 22.9 %fusion.37 = (f32[64,128,128]{1,2,0:T(8,128)}, f32[64,128,128]{1,2,0:T(8,128)}, f32[2,64,128,128]{2,3,1,0:T(8,128)}) fusion(f32[2,32,128,128]{2,3,1,0:T(8,128)} %collective-permute-done, f32[2,32,128,128]{2,3,1,0:T(8,128)S(1)} %copy-done.2, f32[2,128,64,128,1]{3,1,4,2,0:T(8,128)} %fusion.28, f32[64,128,128]{1,2,0:T(8,128)} %copy.40, ...), kind=kOutput, calls=%fused_computation.52 | convolution fusion | flops 3235905536 | bytes 50593792 | tf_op jit(solution)/shard_map/czyx,cdxk->dzyk/dot_general | solution.py:129
  658.7 2.6 slice.33
  661.8 13.3 %collective-permute-done.16 = f32[64,128,128]{1,2,0:T(8,128)} collective-permute-done((f32[64,128,128]{1,2,0:T(8,128)}, f32[64,128,128]{1,2,0:T(8,128)}, u32[]{:S(2)}, u32[]{:S(2)}) %collective-permute-start.16) | collective-permute-done | bytes 4194336 | tf_op jit(solution)/shard_map/ppermute | solution.py:111
  675.2 3.2 add_multiply_fusion.1
  678.3 1.7 fusion.200
  680.1 82.0 %collective-permute-done.18 = f32[64,128,128]{1,2,0:T(8,128)} collective-permute-done((f32[64,128,128]{1,2,0:T(8,128)}, f32[64,128,128]{1,2,0:T(8,128)}, u32[]{:S(2)}, u32[]{:S(2)}) %collective-permute-start.18) | collective-permute-done | bytes 4194336 | tf_op jit(solution)/shard_map/ppermute | solution.py:111
  762.1 3.2 add_multiply_fusion
  765.2 1.7 fusion.201
  767.1 5.0 fusion.74
  777.5 6.6 fusion.75
  784.1 37.6 %collective-permute-done.17 = f32[32,128,128]{1,2,0:T(8,128)S(1)} collective-permute-done((f32[32,128,128]{1,2,0:T(8,128)}, f32[32,128,128]{1,2,0:T(8,128)S(1)}, u32[]{:S(2)}, u32[]{:S(2)}) %collective-permute-start.17) | collective-permute-done | bytes 2097184 | tf_op jit(solution)/shard_map/ppermute | solution.py:20
  821.7 45.0 %collective-permute-done.19 = f32[32,128,128]{1,2,0:T(8,128)} collective-permute-done((f32[32,128,128]{1,2,0:T(8,128)}, f32[32,128,128]{1,2,0:T(8,128)}, u32[]{:S(2)}, u32[]{:S(2)}) %collective-permute-start.19) | collective-permute-done | bytes 2097184 | tf_op jit(solution)/shard_map/ppermute | solution.py:20
  866.8 44.9 %collective-permute-done.21 = f32[32,128,128]{1,2,0:T(8,128)} collective-permute-done((f32[32,128,128]{1,2,0:T(8,128)}, f32[32,128,128]{1,2,0:T(8,128)}, u32[]{:S(2)}, u32[]{:S(2)}) %collective-permute-start.21) | collective-permute-done | bytes 2097184 | tf_op jit(solution)/shard_map/ppermute | solution.py:20
  911.7 44.1 %collective-permute-done.23 = f32[32,128,128]{1,2,0:T(8,128)} collective-permute-done((f32[32,128,128]{1,2,0:T(8,128)}, f32[32,128,128]{1,2,0:T(8,128)}, u32[]{:S(2)}, u32[]{:S(2)}) %collective-permute-start.23) | collective-permute-done | bytes 2097184 | tf_op jit(solution)/shard_map/ppermute | solution.py:20
  955.8 8.7 maximum_select_fusion.1
  964.5 8.9 copy.63
  973.4 9.7 maximum_select_fusion
  983.1 8.9 copy.62
  (101 shorter events, 23.9 us)
Async XLA Ops:
  14.3 157.5 %collective-permute-start.4 = (f32[2,32,128,128]{2,3,1,0:T(8,128)}, f32[2,32,128,128]{2,3,1,0:T(8,128)}, u32[]{:S(2)}, u32[]{:S(2)}) collective-permute-start(f32[2,32,128,128]{2,3,1,0:T(8,128)} %copy.147), channel_id=1, source_target_pairs={{0,2},{1,3},{2,0},{3,1},{4,6},{5,7},{6,4},{7,5},{8,10},{9,11},{10,... | collective-permute-start | bytes 12582920 | tf_op jit(solution)/shard_map/ppermute | solution.py:111
  23.7 51.5 %collective-permute-start.1 = (f32[32,128,128]{2,1,0:T(8,128)}, f32[32,128,128]{2,1,0:T(8,128)}, u32[]{:S(2)}, u32[]{:S(2)}) collective-permute-start(f32[32,128,128]{2,1,0:T(8,128)} %get-tuple-element.14), channel_id=1, source_target_pairs={{28,0},{0,4},{4,8},{8,12},{12,16},{16,20},{20,24},{24,28},{29,1},{... | collective-permute-start | bytes 6291464 | tf_op jit(solution)/shard_map/ppermute | solution.py:20
  25.2 94.9 %collective-permute-start.2 = (f32[32,128,128]{2,1,0:T(8,128)}, f32[32,128,128]{2,1,0:T(8,128)}, u32[]{:S(2)}, u32[]{:S(2)}) collective-permute-start(f32[32,128,128]{2,1,0:T(8,128)} %get-tuple-element.15), channel_id=1, source_target_pairs={{28,0},{0,4},{4,8},{8,12},{12,16},{16,20},{20,24},{24,28},{29,1},{... | collective-permute-start | bytes 6291464 | tf_op jit(solution)/shard_map/ppermute | solution.py:20
  26.7 138.4 %collective-permute-start.9 = (f32[32,128,128]{2,1,0:T(8,128)}, f32[32,128,128]{2,1,0:T(8,128)}, u32[]{:S(2)}, u32[]{:S(2)}) collective-permute-start(f32[32,128,128]{2,1,0:T(8,128)} %get-tuple-element.16), channel_id=1, source_target_pairs={{28,0},{0,4},{4,8},{8,12},{12,16},{16,20},{20,24},{24,28},{29,1},{... | collective-permute-start | bytes 6291464 | tf_op jit(solution)/shard_map/ppermute | solution.py:20
  33.9 198.1 %collective-permute-start = (f32[2,32,128,128]{2,3,1,0:T(8,128)}, f32[2,32,128,128]{2,3,1,0:T(8,128)}, u32[]{:S(2)}, u32[]{:S(2)}) collective-permute-start(f32[2,32,128,128]{2,3,1,0:T(8,128)} %copy.146), channel_id=1, source_target_pairs={{0,1},{1,0},{2,3},{3,2},{4,5},{5,4},{6,7},{7,6},{8,9},{9,8},{10,11... | collective-permute-start | bytes 12582920 | tf_op jit(solution)/shard_map/ppermute | solution.py:111
  75.2 133.5 %collective-permute-start.8 = (f32[32,128,128]{2,1,0:T(8,128)S(1)}, f32[32,128,128]{2,1,0:T(8,128)}, u32[]{:S(2)}, u32[]{:S(2)}) collective-permute-start(f32[32,128,128]{2,1,0:T(8,128)S(1)} %get-tuple-element.17), channel_id=1, source_target_pairs={{28,0},{0,4},{4,8},{8,12},{12,16},{16,20},{20,24},{24,28},{29,1},{... | collective-permute-start | bytes 6291464 | tf_op jit(solution)/shard_map/ppermute | solution.py:20
  120.1 89.1 %collective-permute-start.3 = (f32[32,128,128]{2,1,0:T(8,128)}, f32[32,128,128]{2,1,0:T(8,128)}, u32[]{:S(2)}, u32[]{:S(2)}) collective-permute-start(f32[32,128,128]{2,1,0:T(8,128)} %collective-permute-done.2), channel_id=1, source_target_pairs={{0,1},{1,0},{2,3},{3,2},{4,5},{5,4},{6,7},{7,6},{8,9},{9,8},{10,11... | collective-permute-start | bytes 6291464 | tf_op jit(solution)/shard_map/ppermute | solution.py:111
  165.1 56.0 %collective-permute-start.10 = (f32[32,128,128]{2,1,0:T(8,128)}, f32[32,128,128]{2,1,0:T(8,128)}, u32[]{:S(2)}, u32[]{:S(2)}) collective-permute-start(f32[32,128,128]{2,1,0:T(8,128)} %collective-permute-done.9), channel_id=1, source_target_pairs={{0,1},{1,0},{2,3},{3,2},{4,5},{5,4},{6,7},{7,6},{8,9},{9,8},{10,11... | collective-permute-start | bytes 6291464 | tf_op jit(solution)/shard_map/ppermute | solution.py:111
  171.8 228.8 %collective-permute-start.5 = (f32[2,32,128,128]{2,3,1,0:T(8,128)}, f32[2,32,128,128]{2,3,1,0:T(8,128)}, u32[]{:S(2)}, u32[]{:S(2)}) collective-permute-start(f32[2,32,128,128]{2,3,1,0:T(8,128)} %collective-permute-done.4), channel_id=1, source_target_pairs={{0,1},{1,0},{2,3},{3,2},{4,5},{5,4},{6,7},{7,6},{8,9},{9,8},{10,11... | collective-permute-start | bytes 12582920 | tf_op jit(solution)/shard_map/ppermute | solution.py:111
  208.7 55.2 %collective-permute-start.6 = (f32[32,128,128]{2,1,0:T(8,128)}, f32[32,128,128]{2,1,0:T(8,128)}, u32[]{:S(2)}, u32[]{:S(2)}) collective-permute-start(f32[32,128,128]{2,1,0:T(8,128)} %collective-permute-done.1), channel_id=1, source_target_pairs={{0,2},{1,3},{2,0},{3,1},{4,6},{5,7},{6,4},{7,5},{8,10},{9,11},{10,... | collective-permute-start | bytes 6291464 | tf_op jit(solution)/shard_map/ppermute | solution.py:111
  209.2 148.6 %collective-permute-start.11 = (f32[32,128,128]{2,1,0:T(8,128)}, f32[32,128,128]{2,1,0:T(8,128)}, u32[]{:S(2)}, u32[]{:S(2)}) collective-permute-start(f32[32,128,128]{2,1,0:T(8,128)} %collective-permute-done.8), channel_id=1, source_target_pairs={{0,2},{1,3},{2,0},{3,1},{4,6},{5,7},{6,4},{7,5},{8,10},{9,11},{10,... | collective-permute-start | bytes 6291464 | tf_op jit(solution)/shard_map/ppermute | solution.py:111
  231.4 116.0 %collective-permute-start.7 = (f32[32,128,128]{2,1,0:T(8,128)}, f32[32,128,128]{2,1,0:T(8,128)}, u32[]{:S(2)}, u32[]{:S(2)}) collective-permute-start(f32[32,128,128]{2,1,0:T(8,128)} %collective-permute-done.3), channel_id=1, source_target_pairs={{0,2},{1,3},{2,0},{3,1},{4,6},{5,7},{6,4},{7,5},{8,10},{9,11},{10,... | collective-permute-start | bytes 6291464 | tf_op jit(solution)/shard_map/ppermute | solution.py:111
  232.0 158.2 %collective-permute-start.12 = (f32[32,128,128]{2,1,0:T(8,128)}, f32[32,128,128]{2,1,0:T(8,128)}, u32[]{:S(2)}, u32[]{:S(2)}) collective-permute-start(f32[32,128,128]{2,1,0:T(8,128)} %collective-permute-done.10), channel_id=1, source_target_pairs={{0,2},{1,3},{2,0},{3,1},{4,6},{5,7},{6,4},{7,5},{8,10},{9,11},{10,... | collective-permute-start | bytes 6291464 | tf_op jit(solution)/shard_map/ppermute | solution.py:111
  245.9 6.3 copy-start.1
  245.9 6.3 copy-start.3
  400.6 4.9 copy-start.4
  405.5 11.3 %slice-start = ((s8[8388608]{0:T(1024)(128)(4,1)}), s8[4194304]{0:T(1024)(128)(4,1)S(1)}, s32[]{:S(2)}) async-start(s8[8388608]{0:T(1024)(128)(4,1)} %bitcast.349), calls=%async_computation | async-start | bytes 8388608
  412.4 4.5 slice-start.1
  444.7 16.2 %copy-start.12 = (f32[1,2,64,128]{3,2,0,1:T(8,128)S(1)}, f32[1,2,64,128]{3,2,0,1:T(8,128)}, u32[]{:S(2)}) copy-start(f32[1,2,64,128]{3,2,0,1:T(8,128)} %get-tuple-element.36) | copy-start | bytes 196612
  444.7 16.2 %copy-start.13 = (f32[1,2,64,128]{3,2,0,1:T(8,128)S(1)}, f32[1,2,64,128]{3,2,0,1:T(8,128)}, u32[]{:S(2)}) copy-start(f32[1,2,64,128]{3,2,0,1:T(8,128)} %get-tuple-element.37) | copy-start | bytes 196612
  484.1 22.9 %copy-start.14 = (f32[1,2,128,64]{2,3,0,1:T(8,128)S(1)}, f32[1,2,128,64]{2,3,0,1:T(8,128)}, u32[]{:S(2)}) copy-start(f32[1,2,128,64]{2,3,0,1:T(8,128)} %get-tuple-element.34) | copy-start | bytes 196612
  484.1 22.9 %copy-start.15 = (f32[1,2,128,64]{2,3,0,1:T(8,128)S(1)}, f32[1,2,128,64]{2,3,0,1:T(8,128)}, u32[]{:S(2)}) copy-start(f32[1,2,128,64]{2,3,0,1:T(8,128)} %get-tuple-element.35) | copy-start | bytes 196612
  507.0 13.6 %copy-start = (f32[2,128,128,128]{3,1,2,0:T(8,128)S(1)}, f32[2,128,128,128]{3,1,2,0:T(8,128)}, u32[]{:S(2)}) copy-start(f32[2,128,128,128]{3,1,2,0:T(8,128)} %fusion.9) | copy-start | bytes 50331652
  520.6 9.3 copy-start.9
  529.9 12.3 %copy-start.5 = (f32[2,64,128,128,1]{3,1,2,0,4:T(8,128)S(1)}, f32[2,64,128,128,1]{3,1,2,0,4:T(8,128)}, u32[]{:S(2)}) copy-start(f32[2,64,128,128,1]{3,1,2,0,4:T(8,128)} %fusion.95) | copy-start | bytes 25165828
  542.2 14.0 %copy-start.8 = (f32[2,2,128,128,1]{2,3,1,0,4:T(8,128)S(1)}, f32[2,2,128,128,1]{2,3,1,0,4:T(8,128)}, u32[]{:S(2)}) copy-start(f32[2,2,128,128,1]{2,3,1,0,4:T(8,128)} %get-tuple-element.24) | copy-start | bytes 786436
  542.2 20.3 %slice-start.2 = ((s8[8388608]{0:T(1024)(128)(4,1)}), s8[4194304]{0:T(1024)(128)(4,1)S(1)}, s32[]{:S(2)}) async-start(s8[8388608]{0:T(1024)(128)(4,1)} %bitcast.351), calls=%async_computation.2 | async-start | bytes 8388608
  556.2 6.3 slice-start.3
  562.5 19.6 %copy-start.10 = (f32[1,2,128,64]{2,3,1,0:T(8,128)S(1)}, f32[1,2,128,64]{2,3,1,0:T(8,128)}, u32[]{:S(2)}) copy-start(f32[1,2,128,64]{2,3,1,0:T(8,128)} %get-tuple-element.32) | copy-start | bytes 196612
  562.5 19.6 %copy-start.11 = (f32[1,2,128,64]{2,3,1,0:T(8,128)S(1)}, f32[1,2,128,64]{2,3,1,0:T(8,128)}, u32[]{:S(2)}) copy-start(f32[1,2,128,64]{2,3,1,0:T(8,128)} %get-tuple-element.33) | copy-start | bytes 196612
  581.4 93.8 %collective-permute-start.16 = (f32[64,128,128]{1,2,0:T(8,128)}, f32[64,128,128]{1,2,0:T(8,128)}, u32[]{:S(2)}, u32[]{:S(2)}) collective-permute-start(f32[64,128,128]{1,2,0:T(8,128)} %get-tuple-element.8), channel_id=1, source_target_pairs={{0,2},{1,3},{2,0},{3,1},{4,6},{5,7},{6,4},{7,5},{8,10},{9,11},{10,... | collective-permute-start | bytes 12582920 | tf_op jit(solution)/shard_map/ppermute | solution.py:111
  600.9 161.1 %collective-permute-start.18 = (f32[64,128,128]{1,2,0:T(8,128)}, f32[64,128,128]{1,2,0:T(8,128)}, u32[]{:S(2)}, u32[]{:S(2)}) collective-permute-start(f32[64,128,128]{1,2,0:T(8,128)} %get-tuple-element.9), channel_id=1, source_target_pairs={{0,2},{1,3},{2,0},{3,1},{4,6},{5,7},{6,4},{7,5},{8,10},{9,11},{10,... | collective-permute-start | bytes 12582920 | tf_op jit(solution)/shard_map/ppermute | solution.py:111
  615.5 151.4 %collective-permute-start.14 = (f32[2,32,128,128]{2,3,1,0:T(8,128)}, f32[2,32,128,128]{2,3,1,0:T(8,128)}, u32[]{:S(2)}, u32[]{:S(2)}) collective-permute-start(f32[2,32,128,128]{2,3,1,0:T(8,128)} %slice.35), channel_id=1, source_target_pairs={{0,1},{1,0},{2,3},{3,2},{4,5},{5,4},{6,7},{7,6},{8,9},{9,8},{10,11... | collective-permute-start | bytes 12582920 | tf_op jit(solution)/shard_map/ppermute | solution.py:111
  621.9 13.9 %copy-start.2 = (f32[2,32,128,128]{2,3,1,0:T(8,128)S(1)}, f32[2,32,128,128]{2,3,1,0:T(8,128)}, u32[]{:S(2)}) copy-start(f32[2,32,128,128]{2,3,1,0:T(8,128)} %copy.146) | copy-start | bytes 12582916
  658.6 16.5 %copy-start.7 = (f32[64,128,128]{1,2,0:T(8,128)S(1)}, f32[64,128,128]{1,2,0:T(8,128)}, u32[]{:S(2)}) copy-start(f32[64,128,128]{1,2,0:T(8,128)} %get-tuple-element.10) | copy-start | bytes 12582916
  661.3 112.9 %collective-permute-start.13 = (f32[2,32,128,128]{2,3,1,0:T(8,128)S(1)}, f32[2,32,128,128]{2,3,1,0:T(8,128)}, u32[]{:S(2)}, u32[]{:S(2)}) collective-permute-start(f32[2,32,128,128]{2,3,1,0:T(8,128)S(1)} %slice.33), channel_id=1, source_target_pairs={{0,1},{1,0},{2,3},{3,2},{4,5},{5,4},{6,7},{7,6},{8,9},{9,8},{10,11... | collective-permute-start | bytes 12582920 | tf_op jit(solution)/shard_map/ppermute | solution.py:111
  675.2 86.9 %copy-start.6 = (f32[64,128,128]{1,2,0:T(8,128)S(1)}, f32[64,128,128]{1,2,0:T(8,128)}, u32[]{:S(2)}) copy-start(f32[64,128,128]{1,2,0:T(8,128)} %get-tuple-element.11) | copy-start | bytes 12582916
  680.1 95.5 %collective-permute-start.20 = (f32[32,128,128]{1,2,0:T(8,128)S(1)}, f32[32,128,128]{1,2,0:T(8,128)}, u32[]{:S(2)}, u32[]{:S(2)}) collective-permute-start(f32[32,128,128]{1,2,0:T(8,128)S(1)} %get-tuple-element.21), channel_id=1, source_target_pairs={{0,1},{1,0},{2,3},{3,2},{4,5},{5,4},{6,7},{7,6},{8,9},{9,8},{10,11... | collective-permute-start | bytes 6291464 | tf_op jit(solution)/shard_map/ppermute | solution.py:111
  762.0 4.9 slice-start.4
  762.0 5.1 slice-start.5
  767.0 9.2 collective-permute-start.22
  772.1 201.2 %collective-permute-start.15 = (f32[2,32,128,128]{2,3,1,0:T(8,128)}, f32[2,32,128,128]{2,3,1,0:T(8,128)}, u32[]{:S(2)}, u32[]{:S(2)}) collective-permute-start(f32[2,32,128,128]{2,3,1,0:T(8,128)} %fusion.74), channel_id=1, source_target_pairs={{0,2},{1,3},{2,0},{3,1},{4,6},{5,7},{6,4},{7,5},{8,10},{9,11},{10,... | collective-permute-start | bytes 12582920 | tf_op jit(solution)/shard_map/ppermute | solution.py:111
  773.0 48.7 %collective-permute-start.17 = (f32[32,128,128]{1,2,0:T(8,128)}, f32[32,128,128]{1,2,0:T(8,128)S(1)}, u32[]{:S(2)}, u32[]{:S(2)}) collective-permute-start(f32[32,128,128]{1,2,0:T(8,128)} %get-tuple-element.20), channel_id=1, source_target_pairs={{4,0},{8,4},{12,8},{16,12},{20,16},{24,20},{28,24},{0,28},{5,1},{9... | collective-permute-start | bytes 6291464 | tf_op jit(solution)/shard_map/ppermute | solution.py:20
  774.2 92.6 %collective-permute-start.19 = (f32[32,128,128]{1,2,0:T(8,128)}, f32[32,128,128]{1,2,0:T(8,128)}, u32[]{:S(2)}, u32[]{:S(2)}) collective-permute-start(f32[32,128,128]{1,2,0:T(8,128)} %get-tuple-element.22), channel_id=1, source_target_pairs={{4,0},{8,4},{12,8},{16,12},{20,16},{24,20},{28,24},{0,28},{5,1},{9... | collective-permute-start | bytes 6291464 | tf_op jit(solution)/shard_map/ppermute | solution.py:20
  775.6 136.1 %collective-permute-start.21 = (f32[32,128,128]{1,2,0:T(8,128)}, f32[32,128,128]{1,2,0:T(8,128)}, u32[]{:S(2)}, u32[]{:S(2)}) collective-permute-start(f32[32,128,128]{1,2,0:T(8,128)} %collective-permute-done.20), channel_id=1, source_target_pairs={{4,0},{8,4},{12,8},{16,12},{20,16},{24,20},{28,24},{0,28},{5,1},{9... | collective-permute-start | bytes 6291464 | tf_op jit(solution)/shard_map/ppermute | solution.py:20
  776.1 179.6 %collective-permute-start.23 = (f32[32,128,128]{1,2,0:T(8,128)}, f32[32,128,128]{1,2,0:T(8,128)}, u32[]{:S(2)}, u32[]{:S(2)}) collective-permute-start(f32[32,128,128]{1,2,0:T(8,128)} %collective-permute-done.22), channel_id=1, source_target_pairs={{4,0},{8,4},{12,8},{16,12},{20,16},{24,20},{28,24},{0,28},{5,1},{9... | collective-permute-start | bytes 6291464 | tf_op jit(solution)/shard_map/ppermute | solution.py:20
